TPU v7x, 32 devices: a whole 2x2x4 slice. The times are simulated.
32 devices in a mesh: freq: 8 (over z, x), sens: 4 (over y, core).
Axes of the slice: x: 2, y: 2, z: 4, core: 2. Of those that a mesh axis runs over, the one named last changes fastest.
Arguments:
- samples: bfloat16 [128, 608, 420], P('freq', 'sens'), may hold values from -6 to 6
- response_tiles: bfloat16 [448, 2, 608, 21], P('freq', None, 'sens'), may hold values from -0.25 to 0.25
- slot_sensor: int32 [608], P('sens'), may hold values from -1 to 599, as said below
- sensor_noise: float32 [600], replicated, may hold values from 0.02 to 5
- advance_offset: int32 [21], replicated, may hold values from 0 to 419
Outputs:
- outlook_values: bfloat16 [128, 21, 420], P('freq')
- noise_spread: float32 [21], replicated
Inputs may be any that keep to these rules, and one draw needn't show every extreme that they name: `slot_sensor`: every sensor number appears in exactly one slot; the other 8 slots hold -1.
All inputs are finite; a program needn't handle non-finite values.
Results may differ from a plain program's by a relative error of at most 0.0055.
Values may be sent and summed in bfloat16 or wider, within the bound.
A program may use at most 64 MiB of HBM per device.

v0:
```python
import math
import jax
import jax.numpy as jnp
from jax import lax
from jax.sharding import PartitionSpec as P

KEPT_HARMONICS = 448


def angles(first_bin, bin_count, period, factor):
    bin_index = first_bin + lax.iota(jnp.int32, bin_count)
    turn_count = bin_index[:, None] * factor[None, :] % period
    return turn_count.astype(jnp.float32) * (2.0 * math.pi / period)


def forward_table(bin_count, step_count, period):
    phase_angle = angles(0, bin_count, period, lax.iota(jnp.int32, step_count))
    return jnp.stack([jnp.cos(phase_angle), -jnp.sin(phase_angle)]).astype(jnp.bfloat16)


def inverse_table(bin_count, step_count, period):
    bin_index = lax.iota(jnp.int32, bin_count)
    weight = jnp.where(bin_index == 0, 1.0, 2.0).astype(jnp.float32) / period
    phase_angle = angles(0, bin_count, period, lax.iota(jnp.int32, step_count))
    return jnp.stack(
        [weight[:, None] * jnp.cos(phase_angle), -weight[:, None] * jnp.sin(phase_angle)]
    )


def contract(spectra, blocks):

    def product(left, right):
        return jnp.einsum("krs,ksq->kqr", left, right, preferred_element_type=jnp.float32)

    real_part = product(spectra[0], blocks[:, 0]) - product(spectra[1], blocks[:, 1])
    imag_part = product(spectra[0], blocks[:, 1]) + product(spectra[1], blocks[:, 0])
    return jnp.stack([real_part, imag_part])


def rotate(summed, first_bin, advance_offset, period):
    twiddle = angles(first_bin, summed.shape[1], period, advance_offset)[:, :, None]
    cosine = jnp.cos(twiddle)
    sine_part = jnp.sin(twiddle)
    real_part = summed[0] * cosine - summed[1] * sine_part
    imag_part = summed[0] * sine_part + summed[1] * cosine
    return jnp.stack([real_part, imag_part])


def on_device(samples, response_tiles, slot_sensor, sensor_noise, advance_offset):
    highest = lax.Precision.HIGHEST
    bins_dev = response_tiles.shape[0]
    first_bin = lax.axis_index("freq") * bins_dev
    period = 2 * KEPT_HARMONICS
    step_count = samples.shape[2]
    live_slot = (slot_sensor >= 0).astype(jnp.bfloat16)
    blocks = response_tiles * live_slot[None, None, :, None]
    sensor_ids = lax.iota(jnp.int32, sensor_noise.shape[0])
    slot_noise = jnp.sum(
        jnp.where(
            slot_sensor[:, None] == sensor_ids[None, :], sensor_noise[None, :], jnp.float32(0.0)
        ),
        axis=1,
    )
    wide = blocks.astype(jnp.float32)
    power = wide[:, 0] * wide[:, 0] + wide[:, 1] * wide[:, 1]
    bin_index = first_bin + lax.iota(jnp.int32, bins_dev)
    bin_weight = jnp.where(bin_index == 0, 1.0, 2.0).astype(jnp.float32) / period
    per_bin = jnp.einsum("ksq,s->kq", power, slot_noise, precision=highest)
    noise_spread = lax.psum(jnp.dot(bin_weight, per_bin, precision=highest), ("freq", "sens"))
    forward = forward_table(KEPT_HARMONICS, step_count, period)
    spectra = jnp.einsum(
        "rst,ckt->ckrs", samples, forward, preferred_element_type=jnp.float32
    ).astype(jnp.bfloat16)
    partial_value = contract(spectra, lax.all_gather(blocks, "freq", axis=0, tiled=True))
    base_bin = 0
    backward = inverse_table(KEPT_HARMONICS, step_count, period)
    summed = lax.psum(partial_value, "sens")
    shifted = rotate(summed, base_bin, advance_offset, period)
    kept_entries_local = jnp.einsum("ckqr,ckt->rqt", shifted, backward, precision=highest)
    outlook_values = kept_entries_local.astype(jnp.bfloat16)
    return (outlook_values, noise_spread)


def solution(mesh):
    placed = (P("freq", "sens", None), P("freq", None, "sens", None), P("sens"), P(), P())
    return jax.shard_map(
        on_device,
        mesh=mesh,
        in_specs=placed,
        out_specs=(P("freq", None, None), P()),
        check_vma=False,
    )
```

profile of v0, /device:TPU:0, one launch (start us, length us, event | category | flops | bytes accessed | tf_op | source)
XLA Modules:
  0.0 256.4 jit_solution(4376142394990606409)
XLA Ops:
  7.2 0.0 all-gather.2.cloned.1.call-start
  7.2 0.8 compare_convert_fusion
  8.1 3.6 %fusion.59 = (f32[56,2,152,21]{2,3,0,1:T(8,128)}, bf16[56,2,152,21]{2,3,0,1:T(8,128)(2,1)}) fusion(bf16[152]{0:T(256)(128)(2,1)S(1)} %compare_convert_fusion, bf16[56,2,152,21]{2,1,3,0:T(2,128)(2,1)} %param.6), kind=kLoop, calls=%fused_computation.80 | loop fusion | flops 715008 | bytes 2860336 | tf_op jit(solution)/shard_map/convert_element_type | solution.py:64
  11.7 0.0 all-gather.2.cloned.1.call-update
  11.7 0.0 all-reduce.2.cloned.1.call-start
  11.8 0.2 select_reduce_fusion
  12.0 1.9 fusion.10
  13.9 1.9 fusion.17
  15.8 0.1 copy.35
  15.9 0.1 convolution_bitcast_fusion
  16.1 45.9 %psum.15 = f32[21]{0:T(128)} all-reduce(f32[21]{0:T(128)S(1)} %convolution_bitcast_fusion), channel_id=1, replica_groups=mesh['freq'=8,'sens'=4] {'freq','sens'}, use_global_device_ids=true, to_apply=%region_2.3 | all-reduce | flops 21 | bytes 168 | tf_op jit(solution)/shard_map/psum | solution.py:69
  62.0 3.8 %negate_convert_fusion = (bf16[1,448,420]{1,2,0:T(8,128)(2,1)S(1)}, bf16[1,448,420]{1,2,0:T(8,128)(2,1)S(1)}) fusion(), kind=kLoop, calls=%fused_computation.36 | loop fusion | flops 2257920 | bytes 752640 | tf_op jit(solution)/shard_map/convert.1
  65.8 2.9 %convolution_convert_fusion = bf16[2,448,16,152]{1,3,2,0:T(8,128)(2,1)S(1)} fusion(bf16[16,152,420]{2,1,0:T(8,128)(2,1)S(1)} %copy-done, bf16[1,448,420]{1,2,0:T(8,128)(2,1)S(1)} %get-tuple-element.16, bf16[1,448,420]{1,2,0:T(8,128)(2,1)S(1)} %get-tuple-element.17), kind=kOutput, calls=%fused_computation.8 | convolution fusion | flops 1834104832 | bytes 7153664 | tf_op jit(solution)/shard_map/rst,ckt->ckrs/dot_general | solution.py:71
  68.7 2.6 %slice_bitcast_fusion.7 = (bf16[448,16,152]{0,2,1:T(8,128)(2,1)}, bf16[448,16,152]{0,2,1:T(8,128)(2,1)}) fusion(bf16[2,448,16,152]{1,3,2,0:T(8,128)(2,1)S(1)} %convolution_convert_fusion), kind=kLoop, calls=%fused_computation.10 | loop fusion | bytes 8716288 | tf_op jit(solution)/shard_map/squeeze | solution.py:35
  71.3 7.4 %copy.24 = bf16[448,16,152]{2,1,0:T(8,128)(2,1)} copy(bf16[448,16,152]{0,2,1:T(8,128)(2,1)} %get-tuple-element.8) | data formatting | bytes 4358144 | tf_op jit(solution)/shard_map/squeeze | solution.py:35
  78.8 7.5 %copy.25 = bf16[448,16,152]{2,1,0:T(8,128)(2,1)} copy(bf16[448,16,152]{0,2,1:T(8,128)(2,1)} %get-tuple-element.9) | data formatting | bytes 4358144 | tf_op jit(solution)/shard_map/squeeze | solution.py:35
  86.3 86.1 %all-gather.2.cloned.1.call-done = bf16[448,2,152,21]{2,3,0,1:T(8,128)(2,1)} async-done(((bf16[56,2,152,21]{2,3,0,1:T(8,128)(2,1)}), bf16[448,2,152,21]{2,3,0,1:T(8,128)(2,1)}) %all-gather.2.cloned.1.call-update) | async-done | bytes 5720080 | tf_op jit(solution)/shard_map/all_gather | solution.py:74
  172.4 5.3 %fusion = f32[448,21,16]{1,2,0:T(8,128)S(1)} fusion(bf16[448,16,152]{2,1,0:T(8,128)(2,1)} %copy.25, bf16[448,2,152,21]{2,3,0,1:T(8,128)(2,1)} %all-gather.2.cloned.1.call-done), kind=kOutput, calls=%fused_computation.2 | convolution fusion | flops 45760512 | bytes 9777152 | tf_op jit(solution)/shard_map/krs,ksq->kqr/dot_general | solution.py:33
  177.8 1.4 copy-done.1
  179.2 5.5 %add_bitcast_fusion = f32[1,448,21,16]{2,3,1,0:T(8,128)} fusion(f32[448,21,16]{1,2,0:T(8,128)S(1)} %fusion, bf16[448,16,152]{2,1,0:T(8,128)(2,1)} %copy.24, bf16[448,2,152,21]{2,3,0,1:T(8,128)(2,1)S(1)} %copy-done.1), kind=kOutput, calls=%fused_computation.6 | convolution fusion | flops 45911040 | bytes 11956224 | tf_op jit(solution)/shard_map/krs,ksq->kqr/dot_general | solution.py:33
  184.7 3.0 %copy.29 = f32[1,448,21,16]{1,3,2,0:T(8,128)S(1)} copy(f32[1,448,21,16]{2,3,1,0:T(8,128)} %add_bitcast_fusion) | data formatting | bytes 1204224 | tf_op jit(solution)/shard_map/stack | solution.py:37
  187.7 5.3 %fusion.1 = f32[448,21,16]{1,2,0:T(8,128)S(1)} fusion(bf16[448,16,152]{2,1,0:T(8,128)(2,1)} %copy.24, bf16[448,2,152,21]{2,3,0,1:T(8,128)(2,1)} %all-gather.2.cloned.1.call-done), kind=kOutput, calls=%fused_computation.3 | convolution fusion | flops 45760512 | bytes 9777152 | tf_op jit(solution)/shard_map/krs,ksq->kqr/dot_general | solution.py:33
  193.0 6.1 %subtract_bitcast_fusion = f32[1,448,21,16]{2,3,1,0:T(8,128)} fusion(f32[448,21,16]{1,2,0:T(8,128)S(1)} %fusion.1, bf16[448,16,152]{2,1,0:T(8,128)(2,1)S(1)} %copy-done.2, bf16[448,2,152,21]{2,3,0,1:T(8,128)(2,1)} %all-gather.2.cloned.1.call-done), kind=kOutput, calls=%fused_computation.7 | convolution fusion | flops 45911040 | bytes 8888320 | tf_op jit(solution)/shard_map/krs,ksq->kqr/dot_general | solution.py:33
  199.2 3.7 %copy.28 = f32[1,448,21,16]{1,3,2,0:T(8,128)} copy(f32[1,448,21,16]{2,3,1,0:T(8,128)} %subtract_bitcast_fusion) | data formatting | bytes 1204224 | tf_op jit(solution)/shard_map/stack | solution.py:37
  202.8 2.4 pad_maximum_fusion
  205.2 0.3 fusion.39
  205.5 4.5 %fusion.31 = (f32[1,448,420]{1,2,0:T(8,128)S(1)}, f32[1,448,420]{1,2,0:T(8,128)}) fusion(f32[448]{0:T(512)S(1)} %select_multiply_fusion, f32[448]{0:T(512)S(1)} %fusion.42), kind=kLoop, calls=%fused_computation.43 | loop fusion | flops 2069760 | bytes 1508864 | tf_op jit(solution)/shard_map/mul | solution.py:26
  210.0 33.6 %all-reduce.2.cloned.1.call-done = f32[2,448,21,16]{1,3,2,0:T(8,128)} async-done(((f32[2,448,21,16]{1,3,2,0:T(8,128)}), f32[2,448,21,16]{1,3,2,0:T(8,128)}) %all-reduce.2.cloned.1.call-update) | async-done | bytes 1204240 | tf_op jit(solution)/shard_map/psum | solution.py:77
  243.6 1.6 multiply_subtract_fusion
  245.2 0.1 pad_maximum_fusion.1
  245.3 3.4 %fusion.19 = bf16[16,21,420]{2,1,0:T(8,128)(2,1)S(1)} fusion(f32[2,448,21,16]{1,3,2,0:T(8,128)S(1)} %pad_maximum_fusion.1, f32[1,448,420]{1,2,0:T(8,128)S(1)} %copy-done.3, f32[1,448,420]{1,2,0:T(8,128)S(1)} %get-tuple-element.18), kind=kOutput, calls=%fused_computation.29 | convolution fusion | flops 1517839616 | bytes 2991744 | tf_op jit(solution)/shard_map/ckqr,ckt->rqt/dot_general | solution.py:79
  248.7 0.8 copy.31
  (16 shorter events, 0.1 us)
Async XLA Ops:
  7.2 58.6 %copy-start = (bf16[16,152,420]{2,1,0:T(8,128)(2,1)S(1)}, bf16[16,152,420]{2,1,0:T(8,128)(2,1)}, u32[]{:S(2)}) copy-start(bf16[16,152,420]{2,1,0:T(8,128)(2,1)} %param.5) | copy-start | bytes 6128644
  7.2 165.2 %all-gather.2.cloned.1.call-start = ((), (), s32[]{:S(2)}) async-start(), calls=%async_computation | async-start | bytes 12386304 | tf_op jit(solution)/shard_map/all_gather | solution.py:74
  8.1 3.7 %copy-start.4 = (f32[600]{0:T(1024)S(1)}, f32[600]{0:T(1024)}, u32[]{:S(2)}) copy-start(f32[600]{0:T(1024)} %param.8) | copy-start | bytes 7204
  8.1 3.7 %copy-start.5 = (s32[152]{0:T(256)S(1)}, s32[152]{0:T(256)}, u32[]{:S(2)}) copy-start(s32[152]{0:T(256)} %param.7) | copy-start | bytes 1828
  11.7 231.8 %all-reduce.2.cloned.1.call-start = ((), (), s32[]{:S(2)}) async-start(), calls=%async_computation.1 | async-start | bytes 2752512 | tf_op jit(solution)/shard_map/psum | solution.py:77
  172.4 6.8 %copy-start.1 = (bf16[448,2,152,21]{2,3,0,1:T(8,128)(2,1)S(1)}, bf16[448,2,152,21]{2,3,0,1:T(8,128)(2,1)}, u32[]{:S(2)}) copy-start(bf16[448,2,152,21]{2,3,0,1:T(8,128)(2,1)} %all-gather.2.cloned.1.call-done) | copy-start | bytes 17160196
  187.7 5.4 %copy-start.2 = (bf16[448,16,152]{2,1,0:T(8,128)(2,1)S(1)}, bf16[448,16,152]{2,1,0:T(8,128)(2,1)}, u32[]{:S(2)}) copy-start(bf16[448,16,152]{2,1,0:T(8,128)(2,1)} %copy.25) | copy-start | bytes 6537220
  202.8 2.4 copy-start.6
  243.6 1.7 copy-start.3
Sparse Core Ops, SparseCore 0:
  11.9 160.5 all-gather.1
  205.3 38.1 all-reduce.1
where the time goes:
time: 257 us; the launch traced here: 256 us
  waiting for transfers between devices  120 us (47%)
  blocking collectives  45.9 us (18%)
  matrix products  30.6 us (12%)
  local copies, waits for them, and re-layouts  26.6 us (10%)
  other arithmetic  19.2 us (7%)
  between operations  14.2 us (6%)
    all_gather x1, waiting for transfers between devices, on_device(): lax.all_gather(blocks, 'freq', axis=0, tiled=True)  86.1 us
    psum x1, blocking collectives, on_device(): lax.psum(jnp.dot(bin_weight, per_bin, precision=highest), ('freq', 'sens'))  45.9 us
    psum x1, waiting for transfers between devices, on_device(): summed = lax.psum(partial_value, 'sens')  33.6 us
    dot_general x4, matrix products, product(): jnp.einsum('krs,ksq->kqr', left, right, preferred_element_type=jnp.float32)  22.3 us
    squeeze x2, local copies, waits for them, and re-layouts, contract(): spectra[0]  10 us
    squeeze x1, local copies, waits for them, and re-layouts, contract(): spectra[1]  7.52 us
    another operation x2, local copies, waits for them, and re-layouts, contract(): return jnp.stack([real_part, imag_part])  6.64 us
  transfers between devices with their start and end apart: 2, of which 2 were waited for; matrix products, arithmetic and copies ran while one was open for 13% of the time, Pallas kernels for 0%

commit v1 on v0

--- a/solution.py
+++ b/solution.py
@@ -74,7 +74,9 @@
     partial_value = contract(spectra, lax.all_gather(blocks, "freq", axis=0, tiled=True))
     base_bin = 0
     backward = inverse_table(KEPT_HARMONICS, step_count, period)
-    summed = lax.psum(partial_value, "sens")
+    summed = partial_value
+    for hop in (1, 2):
+        summed = summed + lax.ppermute(summed, "sens", [(dev, dev ^ hop) for dev in range(4)])
     shifted = rotate(summed, base_bin, advance_offset, period)
     kept_entries_local = jnp.einsum("ckqr,ckt->rqt", shifted, backward, precision=highest)
     outlook_values = kept_entries_local.astype(jnp.bfloat16)

time: 257 us -> 294 us (1.14)
  waiting for transfers between devices: 120 us -> 137 us
  blocking collectives: 45.9 us -> 61 us
    all_gather x1, waiting for transfers between devices: 86.1 us -> 135 us  [on_device(): lax.all_gather(blocks, 'freq', axis=0, tiled=True)]
    psum x1 -> x0, waiting for transfers between devices: 33.6 us -> none  [on_device(): summed = lax.psum(partial_value, 'sens')]
    psum x1, blocking collectives: 45.9 us -> 61 us  [on_device(): lax.psum(jnp.dot(bin_weight, per_bin, precision=highest), ('freq', 'sens'))]
    add x0 -> x2, other arithmetic: none -> 5.13 us  [on_device(): summed + lax.ppermute(summed, 'sens', [(dev, dev ^ hop) for dev in range(...]
  transfers between devices with their start and end apart: 2 -> 3, of which waited for: 2 -> 2; matrix products, arithmetic and copies ran while one was open for 13% -> 11% of each run, Pallas kernels for 0% -> 0%
where the time goes in v1:
time: 294 us; the launch traced here: 293 us
  waiting for transfers between devices  137 us (47%)
  blocking collectives  61 us (21%)
  matrix products  30.7 us (10%)
  local copies, waits for them, and re-layouts  26.7 us (9%)
  other arithmetic  22.1 us (8%)
  between operations  14.2 us (5%)
    all_gather x1, waiting for transfers between devices, on_device(): lax.all_gather(blocks, 'freq', axis=0, tiled=True)  135 us
    psum x1, blocking collectives, on_device(): lax.psum(jnp.dot(bin_weight, per_bin, precision=highest), ('freq', 'sens'))  61 us
    dot_general x4, matrix products, product(): jnp.einsum('krs,ksq->kqr', left, right, preferred_element_type=jnp.float32)  22.3 us
    squeeze x2, local copies, waits for them, and re-layouts, contract(): spectra[0]  10.2 us
    squeeze x1, local copies, waits for them, and re-layouts, contract(): spectra[1]  7.42 us
    another operation x2, local copies, waits for them, and re-layouts, contract(): return jnp.stack([real_part, imag_part])  6.66 us
  transfers between devices with their start and end apart: 3, of which 2 were waited for; matrix products, arithmetic and copies ran while one was open for 11% of the time, Pallas kernels for 0%

profile of v1, /device:TPU:0, one launch (start us, length us, event | category | flops | bytes accessed | tf_op | source)
XLA Modules:
  0.0 293.0 jit_solution(11452340311349033262)
XLA Ops:
  7.2 0.8 compare_convert_fusion
  8.1 3.5 %fusion.59 = (f32[56,2,152,21]{2,3,0,1:T(8,128)}, bf16[56,2,152,21]{2,3,0,1:T(8,128)(2,1)}) fusion(bf16[152]{0:T(256)(128)(2,1)S(1)} %compare_convert_fusion, bf16[56,2,152,21]{2,1,3,0:T(2,128)(2,1)} %param.6), kind=kLoop, calls=%fused_computation.80 | loop fusion | flops 715008 | bytes 2860336 | tf_op jit(solution)/shard_map/convert_element_type | solution.py:64
  11.6 3.8 %negate_convert_fusion = (bf16[1,448,420]{1,2,0:T(8,128)(2,1)S(1)}, bf16[1,448,420]{1,2,0:T(8,128)(2,1)S(1)}) fusion(), kind=kLoop, calls=%fused_computation.36 | loop fusion | flops 2257920 | bytes 752640 | tf_op jit(solution)/shard_map/convert.1
  15.4 2.9 %convolution_convert_fusion = bf16[2,448,16,152]{1,3,2,0:T(8,128)(2,1)S(1)} fusion(bf16[16,152,420]{2,1,0:T(8,128)(2,1)S(1)} %copy-done, bf16[1,448,420]{1,2,0:T(8,128)(2,1)S(1)} %get-tuple-element.16, bf16[1,448,420]{1,2,0:T(8,128)(2,1)S(1)} %get-tuple-element.17), kind=kOutput, calls=%fused_computation.8 | convolution fusion | flops 1834104832 | bytes 7153664 | tf_op jit(solution)/shard_map/rst,ckt->ckrs/dot_general | solution.py:71
  18.3 2.6 slice_bitcast_fusion.7
  20.9 7.6 %copy.24 = bf16[448,16,152]{2,1,0:T(8,128)(2,1)} copy(bf16[448,16,152]{0,2,1:T(8,128)(2,1)} %get-tuple-element.8) | data formatting | bytes 4358144 | tf_op jit(solution)/shard_map/squeeze | solution.py:35
  28.5 7.4 %copy.25 = bf16[448,16,152]{2,1,0:T(8,128)(2,1)} copy(bf16[448,16,152]{0,2,1:T(8,128)(2,1)} %get-tuple-element.9) | data formatting | bytes 4358144 | tf_op jit(solution)/shard_map/squeeze | solution.py:35
  35.9 135.4 %all-gather.2.cloned.1.call-done = bf16[448,2,152,21]{2,3,0,1:T(8,128)(2,1)} async-done(((bf16[56,2,152,21]{2,3,0,1:T(8,128)(2,1)}), bf16[448,2,152,21]{2,3,0,1:T(8,128)(2,1)}) %all-gather.2.cloned.1.call-update) | async-done | bytes 5720080 | tf_op jit(solution)/shard_map/all_gather | solution.py:74
  171.4 5.3 %fusion = f32[448,21,16]{1,2,0:T(8,128)S(1)} fusion(bf16[448,16,152]{2,1,0:T(8,128)(2,1)} %copy.25, bf16[448,2,152,21]{2,3,0,1:T(8,128)(2,1)} %all-gather.2.cloned.1.call-done), kind=kOutput, calls=%fused_computation.2 | convolution fusion | flops 45760512 | bytes 9777152 | tf_op jit(solution)/shard_map/krs,ksq->kqr/dot_general | solution.py:33
  176.7 1.4 copy-done.1
  178.2 5.5 %add_bitcast_fusion = f32[1,448,21,16]{2,3,1,0:T(8,128)} fusion(f32[448,21,16]{1,2,0:T(8,128)S(1)} %fusion, bf16[448,16,152]{2,1,0:T(8,128)(2,1)} %copy.24, bf16[448,2,152,21]{2,3,0,1:T(8,128)(2,1)S(1)} %copy-done.1), kind=kOutput, calls=%fused_computation.6 | convolution fusion | flops 45911040 | bytes 11956224 | tf_op jit(solution)/shard_map/krs,ksq->kqr/dot_general | solution.py:33
  183.6 3.0 %copy.29 = f32[1,448,21,16]{1,3,2,0:T(8,128)S(1)} copy(f32[1,448,21,16]{2,3,1,0:T(8,128)} %add_bitcast_fusion) | data formatting | bytes 1204224 | tf_op jit(solution)/shard_map/stack | solution.py:37
  186.6 5.3 %fusion.1 = f32[448,21,16]{1,2,0:T(8,128)S(1)} fusion(bf16[448,16,152]{2,1,0:T(8,128)(2,1)} %copy.24, bf16[448,2,152,21]{2,3,0,1:T(8,128)(2,1)} %all-gather.2.cloned.1.call-done), kind=kOutput, calls=%fused_computation.3 | convolution fusion | flops 45760512 | bytes 9777152 | tf_op jit(solution)/shard_map/krs,ksq->kqr/dot_general | solution.py:33
  192.0 6.1 %subtract_bitcast_fusion = f32[1,448,21,16]{2,3,1,0:T(8,128)} fusion(f32[448,21,16]{1,2,0:T(8,128)S(1)} %fusion.1, bf16[448,16,152]{2,1,0:T(8,128)(2,1)S(1)} %copy-done.2, bf16[448,2,152,21]{2,3,0,1:T(8,128)(2,1)} %all-gather.2.cloned.1.call-done), kind=kOutput, calls=%fused_computation.7 | convolution fusion | flops 45911040 | bytes 8888320 | tf_op jit(solution)/shard_map/krs,ksq->kqr/dot_general | solution.py:33
  198.1 3.7 %copy.28 = f32[1,448,21,16]{1,3,2,0:T(8,128)} copy(f32[1,448,21,16]{2,3,1,0:T(8,128)} %subtract_bitcast_fusion) | data formatting | bytes 1204224 | tf_op jit(solution)/shard_map/stack | solution.py:37
  201.8 2.3 pad_maximum_fusion
  204.1 2.0 fusion.10
  206.2 1.4 collective-permute-done
  207.6 2.7 fusion.60
  210.3 1.5 collective-permute-start.1
  211.8 0.2 select_reduce_fusion
  212.0 1.9 fusion.17
  213.9 0.1 copy.35
  214.0 0.1 convolution_bitcast_fusion
  214.1 61.0 %psum.7 = f32[21]{0:T(128)} all-reduce(f32[21]{0:T(128)S(1)} %convolution_bitcast_fusion), channel_id=1, replica_groups=mesh['freq'=8,'sens'=4] {'freq','sens'}, use_global_device_ids=true, to_apply=%region_1.2 | all-reduce | flops 21 | bytes 168 | tf_op jit(solution)/shard_map/psum | solution.py:69
  275.2 0.3 fusion.39
  275.5 3.6 %fusion.31 = (f32[1,448,420]{1,2,0:T(8,128)S(1)}, f32[1,448,420]{1,2,0:T(8,128)S(1)}) fusion(f32[448]{0:T(512)S(1)} %select_multiply_fusion, f32[448]{0:T(512)S(1)} %fusion.42), kind=kLoop, calls=%fused_computation.43 | loop fusion | flops 2069760 | bytes 1508864 | tf_op jit(solution)/shard_map/mul | solution.py:26
  279.1 2.4 fusion.66
  281.5 0.2 multiply_subtract_fusion
  281.7 0.2 pad_maximum_fusion.1
  281.9 3.4 %fusion.19 = bf16[16,21,420]{2,1,0:T(8,128)(2,1)S(1)} fusion(f32[2,448,21,16]{1,3,2,0:T(8,128)S(1)} %pad_maximum_fusion.1, f32[1,448,420]{1,2,0:T(8,128)S(1)} %get-tuple-element.19, f32[1,448,420]{1,2,0:T(8,128)S(1)} %get-tuple-element.18), kind=kOutput, calls=%fused_computation.29 | convolution fusion | flops 1517839616 | bytes 2991744 | tf_op jit(solution)/shard_map/ckqr,ckt->rqt/dot_general | solution.py:81
  285.3 0.8 copy.31
  (19 shorter events, 0.1 us)
Async XLA Ops:
  7.2 8.2 %copy-start = (bf16[16,152,420]{2,1,0:T(8,128)(2,1)S(1)}, bf16[16,152,420]{2,1,0:T(8,128)(2,1)}, u32[]{:S(2)}) copy-start(bf16[16,152,420]{2,1,0:T(8,128)(2,1)} %param.5) | copy-start | bytes 6128644
  7.2 164.2 %all-gather.2.cloned.1.call-start = ((), (), s32[]{:S(2)}) async-start(), calls=%async_computation | async-start | bytes 12386304 | tf_op jit(solution)/shard_map/all_gather | solution.py:74
  171.4 6.8 %copy-start.1 = (bf16[448,2,152,21]{2,3,0,1:T(8,128)(2,1)S(1)}, bf16[448,2,152,21]{2,3,0,1:T(8,128)(2,1)}, u32[]{:S(2)}) copy-start(bf16[448,2,152,21]{2,3,0,1:T(8,128)(2,1)} %all-gather.2.cloned.1.call-done) | copy-start | bytes 17160196
  186.6 5.4 %copy-start.2 = (bf16[448,16,152]{2,1,0:T(8,128)(2,1)S(1)}, bf16[448,16,152]{2,1,0:T(8,128)(2,1)}, u32[]{:S(2)}) copy-start(bf16[448,16,152]{2,1,0:T(8,128)(2,1)} %copy.25) | copy-start | bytes 6537220
  204.1 3.5 %collective-permute-start = (f32[2,448,21,16]{1,3,2,0:T(8,128)}, f32[2,448,21,16]{1,3,2,0:T(8,128)}, u32[]{:S(2)}, u32[]{:S(2)}) collective-permute-start(f32[2,448,21,16]{1,3,2,0:T(8,128)} %pad_maximum_fusion), channel_id=1, source_target_pairs={{0,1},{1,0},{2,3},{3,2},{4,5},{5,4},{6,7},{7,6},{8,9},{9,8},{10,11... | collective-permute-start | bytes 3612680 | tf_op jit(solution)/shard_map/ppermute | solution.py:79
  204.1 3.5 %copy-start.3 = (f32[1,448,21,16]{1,3,2,0:T(8,128)S(1)}, f32[1,448,21,16]{1,3,2,0:T(8,128)}, u32[]{:S(2)}) copy-start(f32[1,448,21,16]{1,3,2,0:T(8,128)} %copy.28) | copy-start | bytes 1806340
  206.1 5.7 %copy-start.4 = (f32[600]{0:T(1024)S(1)}, f32[600]{0:T(1024)}, u32[]{:S(2)}) copy-start(f32[600]{0:T(1024)} %param.8) | copy-start | bytes 7204
  206.2 5.7 %copy-start.5 = (s32[152]{0:T(256)S(1)}, s32[152]{0:T(256)}, u32[]{:S(2)}) copy-start(s32[152]{0:T(256)} %param.7) | copy-start | bytes 1828
  206.2 69.0 %copy-start.6 = (s32[21]{0:T(128)S(1)}, s32[21]{0:T(128)}, u32[]{:S(2)}) copy-start(s32[21]{0:T(128)} %param.9) | copy-start | bytes 256
  210.3 68.8 %collective-permute-start.1 = (f32[2,448,21,16]{1,3,2,0:T(8,128)}, f32[2,448,21,16]{1,3,2,0:T(8,128)}, u32[]{:S(2)}, u32[]{:S(2)}) collective-permute-start(f32[2,448,21,16]{1,3,2,0:T(8,128)} %fusion.60), channel_id=1, source_target_pairs={{0,2},{1,3},{2,0},{3,1},{4,6},{5,7},{6,4},{7,5},{8,10},{9,11},{10,... | collective-permute-start | bytes 3612680 | tf_op jit(solution)/shard_map/ppermute | solution.py:79
Sparse Core Ops, SparseCore 0:
  11.7 159.6 all-gather.1
